TPU v7x, 32 devices: a whole 2x2x4 slice. The times are simulated.
32 devices in a mesh: dp: 2 (over core), zero: 16 (over z, y, x).
Axes of the slice: x: 2, y: 2, z: 4, core: 2. Of those that a mesh axis runs over, the one named last changes fastest.
Arguments:
- tokens: bfloat16 [32768, 768], P(('dp', 'zero')), may hold values from -6 to 6
- out_grad: bfloat16 [32768, 768], P(('dp', 'zero')), may hold values from -6 to 6
- mask_pos: int32 [256, 32], P(('dp', 'zero')), may hold values from -1 to 127, as said below
- repl_id: int32 [256, 32], P(('dp', 'zero')), may hold values from 0 to 4095
- replace_embed: bfloat16 [4096, 768], replicated, may hold values from -6 to 6
- masters: float32 [16, 768, 768], P(None, 'zero'), as said below
- norm_params: float32 [4, 768], P(None, 'zero'), as said below
- first_moment: float32 [16, 768, 768], P(None, 'zero')
- second_moment: float32 [16, 768, 768], P(None, 'zero'), as said below
- left_basis: float32 [16, 768, 768], P(None, 'zero'), as said below
- right_basis: float32 [16, 768, 768], P(None, 'zero'), as said below
- norm_first: float32 [4, 768], P(None, 'zero')
- norm_second: float32 [4, 768], P(None, 'zero'), as said below
- step: int32 [1], replicated, may hold values from 1 to 20
Outputs:
- layer_out: bfloat16 [32768, 768], P(('dp', 'zero'))
- in_grad: float32 [32768, 768], P(('dp', 'zero'))
- new_first: float32 [16, 768, 768], P(None, 'zero')
- new_second: float32 [16, 768, 768], P(None, 'zero')
- new_master: float32 [16, 768, 768], P(None, 'zero')
- new_copy: bfloat16 [16, 768, 768], P(None, 'zero')
- new_norm_first: float32 [4, 768], P(None, 'zero')
- new_norm_second: float32 [4, 768], P(None, 'zero')
- new_norms: float32 [4, 768], P(None, 'zero')
Inputs may be any that keep to these rules, and one draw needn't show every extreme that they name: `mask_pos`: in each sequence the entries other than -1 are distinct positions and stand in the first slots; a sequence has 1 to 32 of them. `masters`: tiles 0 to 2, the gate and up tiles, tile 3 and the down tiles have entries of deviation about 768^-0.5, (4/768)^0.5, and (2/3072)^0.5. `norm_params`: rows 0 and 2 are gains within 0.7 to 1.3; rows 1 and 3 are shifts. `second_moment`: every entry is positive. `left_basis`: each tile's basis is orthogonal. `right_basis`: each tile's basis is orthogonal. `norm_second`: every entry is positive.
All inputs are finite; a program needn't handle non-finite values.
Results may differ from a plain program's by a relative error of at most 0.0075.
The roundings to bfloat16 on the way count: a program that leaves them out, or rounds other values in their place, can miss the bound.
Values may be sent and summed in bfloat16 or wider, within the bound.
A program may use at most 256 MiB of HBM per device.

v0:
```python
import math
import jax
import jax.numpy as jnp
import numpy as np
from jax import lax
from jax.sharding import PartitionSpec as P

HEADS = 12
CAP = 1
highest = lax.Precision.HIGHEST
norm_eps = 1e-12
beta_one = 0.9
beta_two = 0.95
adam_eps = 1e-08
peak_rate = 0.1
warm_steps = 5.0
total_steps = 60.0
decay_rate = 0.01


def alibi_slopes(head_count):

    def power_slopes(power_count):
        first_slope = 2.0 ** (-8.0 / power_count)
        return [first_slope ** (position + 1) for position in range(power_count)]

    nearest = 2 ** int(math.floor(math.log2(head_count)))
    slope_list = power_slopes(nearest)
    slope_list = slope_list + power_slopes(2 * nearest)[0::2][: head_count - nearest]
    return np.array(slope_list, np.float32)


def layer_norm(values, gain_row, shift_row):
    row_mean = jnp.mean(values, axis=-1, keepdims=True)
    centered = values - row_mean
    spread = jnp.mean(centered * centered, axis=-1, keepdims=True)
    return centered * lax.rsqrt(spread + norm_eps) * gain_row + shift_row


def gated(gate_val, up_value):
    return jax.nn.gelu(gate_val, approximate=False) * up_value


def shards(
    tokens,
    out_grad,
    mask_pos,
    repl_id,
    replace_embed,
    masters,
    norm_params,
    first_moment,
    second_moment,
    left_basis,
    right_basis,
    norm_first,
    norm_second,
    step,
):
    seq_count = mask_pos.shape[0]
    tok_rows, model_width = tokens.shape
    length = tok_rows // seq_count
    head_count = HEADS
    head_size = model_width // head_count
    score_scale = float(head_size) ** (-0.5)
    tile_count = masters.shape[0]
    ff_parts = (tile_count - 4) // 3
    shard_rows = masters.shape[1]
    positions = jnp.arange(length, dtype=jnp.int32)
    mask_hits = mask_pos[:, :, None] == positions[None, None, :]
    masked = jnp.any(mask_hits, axis=1).reshape(-1, 1)
    row_ids = jnp.sum(jnp.where(mask_hits, repl_id[:, :, None], 0), axis=1).reshape(-1)
    inputs = jnp.where(masked, jnp.take(replace_embed, row_ids, axis=0), tokens)
    shard_low = masters.astype(jnp.bfloat16)
    whole_tiles, norm_whole = (
        lax.all_gather(shard_low, "zero", axis=1, tiled=True),
        lax.all_gather(norm_params.astype(jnp.bfloat16), "zero", axis=1, tiled=True),
    )
    norm_gains = norm_whole.astype(jnp.float32)
    slopes = jnp.asarray(alibi_slopes(head_count))
    distance = jnp.abs(positions[:, None] - positions[None, :]).astype(jnp.float32)
    alibi_bias = -slopes[:, None, None] * distance[None]
    head_shape = (seq_count, length, head_count, head_size)
    qkv_low = jnp.einsum(
        "td,kde->kte", inputs, whole_tiles[0:3], preferred_element_type=jnp.float32
    ).astype(jnp.bfloat16)
    queries = qkv_low[0].reshape(head_shape)
    key_rows = qkv_low[1].reshape(head_shape)
    values = qkv_low[2].reshape(head_shape)

    def score_block():
        raw_scores = jnp.einsum(
            "bqhd,bkhd->bhqk", queries, key_rows, preferred_element_type=jnp.float32
        )
        return raw_scores * score_scale + alibi_bias[None]

    scores = score_block()
    row_max = jnp.max(scores, axis=-1, keepdims=True)
    log_total = row_max + jnp.log(jnp.sum(jnp.exp(scores - row_max), axis=-1, keepdims=True))
    soft_low = jnp.exp(scores - log_total).astype(jnp.bfloat16)
    mixed_low = jnp.einsum("bhqk,bkhd->bqhd", soft_low, values, preferred_element_type=jnp.float32)
    mixed_low = mixed_low.reshape(tok_rows, model_width).astype(jnp.bfloat16)
    attended = jnp.dot(mixed_low, whole_tiles[3], preferred_element_type=jnp.float32)
    first_sum = inputs.astype(jnp.float32) + attended
    hidden, first_back = jax.vjp(layer_norm, first_sum, norm_gains[0], norm_gains[1])
    hidden_low = hidden.astype(jnp.bfloat16)
    gate_up = jnp.einsum(
        "td,fde->tfe",
        hidden_low,
        whole_tiles[4 : 4 + 2 * ff_parts],
        preferred_element_type=jnp.float32,
    )
    gate_val = gate_up[:, :ff_parts].reshape(tok_rows, ff_parts * model_width)
    up_value = gate_up[:, ff_parts:].reshape(tok_rows, ff_parts * model_width)
    inner_act, inner_back = jax.vjp(gated, gate_val, up_value)
    inner_low = inner_act.astype(jnp.bfloat16).reshape(tok_rows, ff_parts, model_width)
    branch = jnp.einsum(
        "tfe,fed->td",
        inner_low,
        whole_tiles[4 + 2 * ff_parts :],
        preferred_element_type=jnp.float32,
    )
    layer_out, second_back = jax.vjp(layer_norm, hidden + branch, norm_gains[2], norm_gains[3])
    back_tiles = lax.all_gather(shard_low, "zero", axis=1, tiled=True)
    d_second, d_gain_two, d_shift_two = second_back(out_grad.astype(jnp.float32))
    d_branch = d_second.astype(jnp.bfloat16)
    grad_down = jnp.einsum("tfe,td->fed", inner_low, d_branch, preferred_element_type=jnp.float32)
    d_inner = jnp.einsum(
        "td,fed->tfe", d_branch, back_tiles[4 + 2 * ff_parts :], preferred_element_type=jnp.float32
    )
    d_gate, d_up = inner_back(d_inner.reshape(tok_rows, ff_parts * model_width))
    d_gate_up = jnp.concatenate(
        [
            d_gate.reshape(tok_rows, ff_parts, model_width),
            d_up.reshape(tok_rows, ff_parts, model_width),
        ],
        axis=1,
    ).astype(jnp.bfloat16)
    grad_gate_up = jnp.einsum(
        "td,tfe->fde", hidden_low, d_gate_up, preferred_element_type=jnp.float32
    )
    d_hidden = d_second + jnp.einsum(
        "tfe,fde->td",
        d_gate_up,
        back_tiles[4 : 4 + 2 * ff_parts],
        preferred_element_type=jnp.float32,
    )
    d_first, d_gain_one, d_shift_one = first_back(d_hidden)
    d_attended = d_first.astype(jnp.bfloat16)
    grad_out = jnp.einsum("td,te->de", mixed_low, d_attended, preferred_element_type=jnp.float32)
    d_mixed = jnp.einsum("te,de->td", d_attended, back_tiles[3], preferred_element_type=jnp.float32)
    d_mixed = d_mixed.astype(jnp.bfloat16).reshape(head_shape)
    again_probs = jnp.exp(score_block() - log_total)
    again_low = again_probs.astype(jnp.bfloat16)
    d_probs = jnp.einsum("bqhd,bkhd->bhqk", d_mixed, values, preferred_element_type=jnp.float32)
    row_delta = jnp.sum(again_probs * d_probs, axis=-1, keepdims=True)
    d_scores = (again_probs * (d_probs - row_delta)).astype(jnp.bfloat16)
    d_query = (
        jnp.einsum("bhqk,bkhd->bqhd", d_scores, key_rows, preferred_element_type=jnp.float32)
        * score_scale
    )
    d_keys = (
        jnp.einsum("bhqk,bqhd->bkhd", d_scores, queries, preferred_element_type=jnp.float32)
        * score_scale
    )
    d_values = jnp.einsum("bhqk,bqhd->bkhd", again_low, d_mixed, preferred_element_type=jnp.float32)
    d_qkv = (
        jnp.stack([d_query, d_keys, d_values])
        .reshape(3, tok_rows, model_width)
        .astype(jnp.bfloat16)
    )
    grad_qkv = jnp.einsum("td,kte->kde", inputs, d_qkv, preferred_element_type=jnp.float32)
    d_inputs = d_first + jnp.einsum(
        "kte,kde->td", d_qkv, back_tiles[0:3], preferred_element_type=jnp.float32
    )
    in_grad = jnp.where(masked, 0.0, d_inputs)
    tile_grads = jnp.concatenate([grad_qkv, grad_out[None], grad_gate_up, grad_down], axis=0)
    norm_grads = jnp.stack([d_gain_one, d_shift_one, d_gain_two, d_shift_two])
    step_value = step[0].astype(jnp.float32)
    step_rate = peak_rate * jnp.minimum(
        step_value / warm_steps, (total_steps - step_value) / (total_steps - warm_steps)
    )
    fix_one = 1.0 - jnp.power(beta_one, step_value)
    fix_two = 1.0 - jnp.power(beta_two, step_value)
    devices = lax.axis_size("zero")
    capacity = CAP
    target = jnp.arange(tile_count, dtype=jnp.int32)
    slot_index = jnp.arange(devices * capacity, dtype=jnp.int32)
    source = jnp.where(slot_index < tile_count, slot_index, 0)

    def outgoing(source_array):
        return jnp.take(source_array, source, axis=0).reshape(
            devices, capacity, shard_rows, model_width
        )

    tile_sum, norm_sum = (
        lax.psum_scatter(tile_grads, "zero", scatter_dimension=1, tiled=True),
        lax.psum_scatter(norm_grads, "zero", scatter_dimension=1, tiled=True),
    )
    tile_sum, norm_sum = lax.psum((tile_sum, norm_sum), "dp")
    left_whole = lax.all_to_all(
        outgoing(left_basis), "zero", split_axis=0, concat_axis=2, tiled=True
    )
    right_whole = lax.all_to_all(
        outgoing(right_basis), "zero", split_axis=0, concat_axis=2, tiled=True
    )
    rotated = jnp.einsum(
        "akji,akjl->akil",
        left_whole,
        lax.all_to_all(outgoing(tile_sum), "zero", split_axis=0, concat_axis=2, tiled=True),
        precision=highest,
    )
    rotated = jnp.einsum("akil,aklm->akim", rotated, right_whole, precision=highest)
    moment_one = (
        beta_one
        * lax.all_to_all(outgoing(first_moment), "zero", split_axis=0, concat_axis=2, tiled=True)
        + (1.0 - beta_one) * rotated
    )
    moment_two = (
        beta_two
        * lax.all_to_all(outgoing(second_moment), "zero", split_axis=0, concat_axis=2, tiled=True)
        + (1.0 - beta_two) * rotated * rotated
    )
    direction = moment_one / fix_one / (jnp.sqrt(moment_two / fix_two) + adam_eps)
    update = jnp.einsum("akij,akjl->akil", left_whole, direction, precision=highest)
    update = jnp.einsum("akil,akml->akim", update, right_whole, precision=highest)
    results = jnp.stack([moment_one, moment_two, update], axis=2)
    returned = lax.all_to_all(results, "zero", split_axis=3, concat_axis=0, tiled=True)
    returned = returned.reshape(devices * capacity, 3, shard_rows, model_width)
    owned_back = jnp.take(returned, target, axis=0)
    new_master = masters - step_rate * (owned_back[:, 2] + decay_rate * masters)
    new_norm_first = beta_one * norm_first + (1.0 - beta_one) * norm_sum
    new_norm_second = beta_two * norm_second + (1.0 - beta_two) * norm_sum * norm_sum
    new_norms = norm_params - step_rate * (new_norm_first / fix_one) / (
        jnp.sqrt(new_norm_second / fix_two) + adam_eps
    )
    return (
        layer_out.astype(jnp.bfloat16),
        in_grad,
        owned_back[:, 0],
        owned_back[:, 1],
        new_master,
        new_master.astype(jnp.bfloat16),
        new_norm_first,
        new_norm_second,
        new_norms,
    )


def solution(mesh):
    in_specs = (
        P(("dp", "zero"), None),
        P(("dp", "zero"), None),
        P(("dp", "zero"), None),
        P(("dp", "zero"), None),
        P(),
        P(None, "zero", None),
        P(None, "zero"),
        P(None, "zero", None),
        P(None, "zero", None),
        P(None, "zero", None),
        P(None, "zero", None),
        P(None, "zero"),
        P(None, "zero"),
        P(),
    )
    out_specs = (
        P(("dp", "zero"), None),
        P(("dp", "zero"), None),
        P(None, "zero", None),
        P(None, "zero", None),
        P(None, "zero", None),
        P(None, "zero", None),
        P(None, "zero"),
        P(None, "zero"),
        P(None, "zero"),
    )
    return jax.shard_map(shards, mesh=mesh, in_specs=in_specs, out_specs=out_specs, check_vma=False)
```

profile of v0, /device:TPU:0, one launch (start us, length us, event | category | flops | bytes accessed | tf_op | source)
XLA Modules:
  0.0 1709.1 jit_solution(17990816463985661530)
XLA Ops:
  15.6 9.2 gather_fusion
  27.4 43.7 %all-gather = bf16[16,48,4]{1,2,0:T(4,128)(2,1)S(1)} all-gather(bf16[1,48,4]{1,2,0:T(4,128)(2,1)S(1)} %convert_bitcast_fusion.1), channel_id=1, replica_groups=mesh['dp'=2,'zero'=16] {'zero'}, dimensions={0}, use_global_device_ids=true | all-gather | bytes 6528 | tf_op jit(solution)/shard_map/all_gather | solution.py:77
  74.8 150.4 %all-gather.3.cloned.1.call-done = bf16[16,768,768]{2,1,0:T(8,128)(2,1)} async-done(((bf16[16,48,768]{2,1,0:T(8,128)(2,1)}), bf16[16,768,768]{2,1,0:T(8,128)(2,1)}) %all-gather.3.cloned.1.call-update) | async-done | bytes 18874384 | tf_op jit(solution)/shard_map/all_gather | solution.py:76
  225.2 6.4 convert_bitcast_fusion
  260.9 19.5 %fusion.9 = f32[1024,8,768]{2,0,1:T(8,128)} fusion(bf16[16,768,768]{2,1,0:T(8,128)(2,1)} %all-gather.3.cloned.1.call-done, f32[1024,768]{0,1:T(8,128)S(1)} %get-tuple-element.114, f32[768]{0:T(1024)S(1)} %get-tuple-element.83, f32[768]{0:T(1024)S(1)} %get-tuple-element.84, f32[1024]{0:T(1024)S(1)} %fusion.81, f32[1024]{0:T(1024)S(1)} %broadcast_multiply_fusion.4), kind=kOutput, calls=%fused_computation.31 | convolution fusion | flops 9667608576 | bytes 37763072 | tf_op jit(solution)/shard_map/td,fde->tfe/dot_general | solution.py:107
  280.4 29.9 %multiply_convert_fusion.1 = (bf16[1024,4,768]{2,0,1:T(8,128)(2,1)S(1)}, f32[1024,4,768]{2,0,1:T(8,128)}) fusion(f32[1024,8,768]{2,0,1:T(8,128)} %fusion.9), kind=kLoop, calls=%fused_computation.13 | loop fusion | flops 207618048 | bytes 44040192 | tf_op jit(solution)/shard_map/convert_element_type | solution.py:116
  310.4 9.3 fusion.101
  324.2 24.4 %add_convert_fusion = (bf16[1024,4,768]{2,0,1:T(8,128)(2,1)}, bf16[1024,4,768]{2,0,1:T(8,128)(2,1)}) fusion(f32[1024,4,768]{2,0,1:T(8,128)} %get-tuple-element.93, f32[1024,8,768]{2,0,1:T(8,128)} %fusion.9, bf16[16,768,768]{2,1,0:T(8,128)(2,1)} %all-gather.3.cloned.1.call-done, f32[1024]{0:T(1024)S(1)} %negate_multiply_fusion.2, ...), kind=kOutput, calls=%fused_computation.12 | convolution fusion | flops 4895539200 | bytes 59788288 | tf_op jit(solution)/shard_map/td,fed->tfe/dot_general | solution.py:128
  348.6 24.5 %multiply_reduce_fusion.1 = (f32[768]{0:T(1024)}, f32[1024]{0:T(1024)S(1)}, f32[768]{0:T(1024)}, f32[1024,768]{0,1:T(8,128)}) fusion(f32[1024,768]{0,1:T(8,128)} %copy-done.12, f32[1024]{0:T(1024)S(1)} %fusion.81, f32[1024]{0:T(1024)S(1)} %broadcast_multiply_fusion.4, f32[768]{0:T(1024)S(1)} %get-tuple-element.84, ...), kind=kOutput, calls=%fused_computation.65 | convolution fusion | flops 9683334144 | bytes 33071104 | tf_op jit(solution)/shard_map/tfe,fde->td/dot_general | solution.py:142
  405.7 8.2 fusion.77
  413.9 18.5 %fusion.12 = f32[8,768,768]{1,2,0:T(8,128)} fusion(bf16[1024,4,768]{2,0,1:T(8,128)(2,1)} %get-tuple-element.95, bf16[1024,4,768]{2,0,1:T(8,128)(2,1)} %get-tuple-element.94, f32[1024,768]{0,1:T(8,128)} %copy-done.12, f32[768]{0:T(1024)S(1)} %get-tuple-element.83, f32[768]{0:T(1024)S(1)} %get-tuple-element.84, f32[1024]{0:T(1024)S(1)} %fusion.81, ...), kind=kOutput, calls=%fused_computation.34 | convolution fusion | flops 9673900032 | bytes 34617344 | tf_op jit(solution)/shard_map/td,tfe->fde/dot_general | solution.py:139
  432.4 5.2 convolution_bitcast_fusion.2
  466.6 9.7 convolution_bitcast_fusion
  476.3 26.0 %pad_maximum_fusion = f32[16,768,768]{1,2,0:T(8,128)} fusion(f32[4,768,768]{1,2,0:T(8,128)} %fusion.77, f32[8,768,768]{1,2,0:T(8,128)} %fusion.12, f32[1,768,768]{1,2,0:T(8,128)} %convolution_bitcast_fusion.2, f32[3,768,768]{1,2,0:T(8,128)} %convolution_bitcast_fusion), kind=kLoop, calls=%fused_computation.7 | loop fusion | flops 28311552 | bytes 75497472 | tf_op jit(solution)/shard_map/concatenate | solution.py:177
  502.2 37.9 %copy.333 = f32[16,768,768]{2,0,1:T(8,128)} copy(f32[16,768,768]{1,2,0:T(8,128)} %pad_maximum_fusion) | data formatting | bytes 75497472 | tf_op jit(solution)/shard_map/concatenate | solution.py:177
  540.3 538.9 %reduce-scatter.5.cloned.1.call-done = f32[16,48,768]{2,0,1:T(8,128)} async-done(((f32[16,768,768]{2,0,1:T(8,128)}), f32[16,48,768]{2,0,1:T(8,128)}) %reduce-scatter.5.cloned.1.call-update) | async-done | bytes 2359312 | tf_op jit(solution)/shard_map/reduce_scatter | solution.py:197
  1097.2 7.6 all-reduce.2.cloned.1.call-done
  1108.5 7.8 select_bitcast_fusion
  1116.4 62.3 %all_to_all.60 = f32[16,1,48,768]{3,2,1,0:T(8,128)} all-to-all(f32[16,1,48,768]{3,2,1,0:T(8,128)} %get-tuple-element.107), channel_id=1, replica_groups=mesh['dp'=2,'zero'=16] {'zero'}, dimensions={0} | all-to-all | bytes 4718592 | tf_op jit(solution)/shard_map/all_to_all | solution.py:201
  1178.7 57.7 %all_to_all.61 = f32[16,1,48,768]{3,2,1,0:T(8,128)} all-to-all(f32[16,1,48,768]{3,2,1,0:T(8,128)S(1)} %get-tuple-element.106), channel_id=1, replica_groups=mesh['dp'=2,'zero'=16] {'zero'}, dimensions={0} | all-to-all | bytes 4718592 | tf_op jit(solution)/shard_map/all_to_all | solution.py:221
  1236.4 57.8 %all_to_all.62 = f32[16,1,48,768]{3,2,1,0:T(8,128)} all-to-all(f32[16,1,48,768]{3,2,1,0:T(8,128)S(1)} %get-tuple-element.110), channel_id=1, replica_groups=mesh['dp'=2,'zero'=16] {'zero'}, dimensions={0} | all-to-all | bytes 4718592 | tf_op jit(solution)/shard_map/all_to_all | solution.py:216
  1294.2 57.8 %all_to_all.63 = f32[16,1,48,768]{3,2,1,0:T(8,128)} all-to-all(f32[16,1,48,768]{3,2,1,0:T(8,128)S(1)} %get-tuple-element.108), channel_id=1, replica_groups=mesh['dp'=2,'zero'=16] {'zero'}, dimensions={0} | all-to-all | bytes 4718592 | tf_op jit(solution)/shard_map/all_to_all | solution.py:210
  1364.3 7.7 fusion.37
  1372.0 31.2 %all-to-all-done.3 = f32[16,1,48,768]{3,2,1,0:T(8,128)} async-done(((f32[16,1,48,768]{3,2,1,0:T(8,128)}), f32[16,1,48,768]{3,2,1,0:T(8,128)}, u32[]{:S(2)}, u32[]{:S(2)}) %all-to-all-start.3) | async-done | bytes 2359328 | tf_op jit(solution)/shard_map/all_to_all | solution.py:204
  1403.1 10.2 fusion.31
  1413.4 6.5 fusion.40
  1419.9 7.9 convolution_bitcast_fusion.1
  1428.3 10.4 copy.336
  1438.6 10.9 all-to-all-start.5
  1450.7 10.0 fusion.23
  1466.9 209.3 %reduce-scatter.7.cloned.1.call-done = f32[48,4]{1,0:T(8,128)} async-done(((f32[768,4]{1,0:T(8,128)}), f32[48,4]{1,0:T(8,128)}) %reduce-scatter.7.cloned.1.call-update) | async-done | bytes 784
  1687.0 7.0 gather_fusion.1
  (178 shorter events, 169.8 us)
Async XLA Ops:
  7.2 1076.4 %copy-start = (f32[16,48,768]{2,1,0:T(8,128)S(1)}, f32[16,48,768]{2,1,0:T(8,128)}, u32[]{:S(2)}) copy-start(f32[16,48,768]{2,1,0:T(8,128)} %param.25) | copy-start | bytes 7077892
  7.2 218.0 %all-gather.3.cloned.1.call-start = ((), (), s32[]{:S(2)}) async-start(), calls=%async_computation.8 | async-start | bytes 20054016 | tf_op jit(solution)/shard_map/all_gather | solution.py:76
  10.2 5.2 copy-start.24
  10.2 5.2 copy-start.27
  10.2 1068.9 %reduce-scatter.5.cloned.1.call-start = ((), (), s32[]{:S(2)}) async-start(), calls=%async_computation.9 | async-start | bytes 40108032 | tf_op jit(solution)/shard_map/reduce_scatter | solution.py:197
  24.8 46.6 %copy-start.34 = (f32[12]{0:T(128)S(1)}, f32[12]{0:T(128)}, u32[]{:S(2)}) copy-start(f32[12]{0:T(128)} %constant.173) | copy-start | bytes 148
  71.3 160.2 %copy-start.30 = (pred[8,128]{1,0:T(8,128)(4,1)}, pred[8,128]{1,0:T(8,128)(4,1)S(1)}, u32[]{:S(2)}) copy-start(pred[8,128]{1,0:T(8,128)(4,1)S(1)} %fusion.80) | copy-start | bytes 3076
  257.1 3.4 copy-start.20
  260.5 49.8 %copy-start.12 = (f32[1024,768]{0,1:T(8,128)}, f32[1024,768]{0,1:T(8,128)S(1)}, u32[]{:S(2)}) copy-start(f32[1024,768]{0,1:T(8,128)S(1)} %get-tuple-element.114) | copy-start | bytes 9437188
  310.4 9.4 copy-start.15
  310.4 9.4 copy-start.6
  319.8 4.4 copy-start.10
  387.2 5.2 copy-start.9
  387.2 9.8 slice-start
  392.4 4.6 slice-start.1
  392.4 12.5 slice-start.2
  397.0 7.9 slice-start.3
  399.3 3.4 copy-start.3
  540.2 564.6 %all-reduce.2.cloned.1.call-start = ((), (), s32[]{:S(2)}) async-start(), calls=%async_computation.10 | async-start | bytes 4718592 | tf_op jit(solution)/shard_map/psum | solution.py:200
  1352.0 51.1 %all-to-all-start.3 = ((f32[16,1,48,768]{3,2,1,0:T(8,128)}), f32[16,1,48,768]{3,2,1,0:T(8,128)}, u32[]{:S(2)}, u32[]{:S(2)}) async-start(f32[16,1,48,768]{3,2,1,0:T(8,128)} %get-tuple-element.109), calls=%async_computation.4 | async-start | bytes 4718592 | tf_op jit(solution)/shard_map/all_to_all | solution.py:204
  1356.9 4.2 copy-start.13
  1403.1 10.2 copy-start.18
  1438.6 11.0 copy-start.23
  1438.6 11.0 copy-start.22
  1438.6 11.0 copy-start.29
  1438.6 11.1 copy-start.28
  1438.6 12.1 copy-start.31
  1438.6 241.4 %all-to-all-start.5 = ((f32[1,1,3,768,768]{4,1,2,0,3:T(1,128)}), f32[1,1,3,768,768]{4,1,2,0,3:T(1,128)}, u32[]{:S(2)}, u32[]{:S(2)}) async-start(f32[1,1,3,768,768]{4,1,2,0,3:T(1,128)} %copy.336), calls=%async_computation.6 | async-start | bytes 14155776 | tf_op jit(solution)/shard_map/all_to_all | solution.py:228
  1449.5 226.6 %reduce-scatter.7.cloned.1.call-start = ((), (), s32[]{:S(2)}) async-start(), calls=%async_computation.11 | async-start | bytes 417792
  1463.3 216.1 %copy-start.26 = (f32[4,48]{1,0:T(4,128)S(1)}, f32[4,48]{1,0:T(4,128)}, u32[]{:S(2)}) copy-start(f32[4,48]{1,0:T(4,128)} %param.23) | copy-start | bytes 2308
  1463.3 216.1 %copy-start.32 = (f32[4,48]{1,0:T(4,128)S(1)}, f32[4,48]{1,0:T(4,128)}, u32[]{:S(2)}) copy-start(f32[4,48]{1,0:T(4,128)} %param.29) | copy-start | bytes 2308
  1463.3 216.1 %copy-start.33 = (f32[4,48]{1,0:T(4,128)S(1)}, f32[4,48]{1,0:T(4,128)}, u32[]{:S(2)}) copy-start(f32[4,48]{1,0:T(4,128)} %param.28) | copy-start | bytes 2308
  (13 other events, 30.3 us)
Sparse Core Ops, SparseCore 0:
  11.3 213.8 all-gather.2
  540.3 538.7 reduce-scatter.4
  1083.7 21.0 all-reduce.1
  1455.2 220.8 reduce-scatter.6
where the time goes:
time: 1720 us; the launch traced here: 1710 us
  waiting for transfers between devices  937 us (54%)
  blocking collectives  282 us (16%)
  matrix products  194 us (11%)
  local copies, waits for them, and re-layouts  170 us (10%)
  other arithmetic  94.5 us (5%)
    reduce_scatter x1, waiting for transfers between devices, shards(): lax.psum_scatter(tile_grads, 'zero', scatter_dimension=1, tiled=True)  539 us
    unnamed x5, waiting for transfers between devices  209 us
    all_gather x1, waiting for transfers between devices, shards(): lax.all_gather(shard_low, 'zero', axis=1, tiled=True)  150 us
    all_to_all x1, blocking collectives, shards(): lax.all_to_all(outgoing(left_basis), 'zero', split_axis=0, concat_axis=2,...  62.3 us
    all_to_all x1, blocking collectives, shards(): lax.all_to_all(outgoing(first_moment), 'zero', split_axis=0, concat_axis=...  57.8 us
    all_to_all x1, blocking collectives, shards(): lax.all_to_all(outgoing(tile_sum), 'zero', split_axis=0, concat_axis=2, t...  57.8 us
    all_to_all x1, blocking collectives, shards(): lax.all_to_all(outgoing(second_moment), 'zero', split_axis=0, concat_axis...  57.7 us
    all_gather x1, blocking collectives, shards(): lax.all_gather(norm_params.astype(jnp.bfloat16), 'zero', axis=1, tiled=True)  43.7 us
  transfers between devices with their start and end apart: 6, of which 5 were waited for; matrix products, arithmetic and copies ran while one was open for 4% of the time, Pallas kernels for 0%

commit v1 on v0

--- a/solution.py
+++ b/solution.py
@@ -16,6 +16,28 @@
 warm_steps = 5.0
 total_steps = 60.0
 decay_rate = 0.01
+
+
+def in_order(parts, dim):
+    shape = list(parts.shape[1:])
+    shape[dim] *= parts.shape[0]
+    return jnp.moveaxis(parts, 0, dim).reshape(shape)
+
+
+def grow_blocks(value, axis):
+    size = lax.axis_size(axis)
+    blocks = value[None]
+    for level in range(size.bit_length() - 1):
+        distance = 1 << level
+        partner_block = lax.ppermute(blocks, axis, [(i, i ^ distance) for i in range(size)])
+        both = jnp.stack([blocks, partner_block])
+        upper = lax.axis_index(axis) >> level & 1
+        blocks = jnp.where(upper == 0, both, both[::-1]).reshape(-1, *value.shape)
+    return blocks
+
+
+def gather_by_bits(x, axis, dim):
+    return in_order(grow_blocks(x, axis), dim)
 
 
 def alibi_slopes(head_count):
@@ -74,7 +96,7 @@
     shard_low = masters.astype(jnp.bfloat16)
     whole_tiles, norm_whole = (
         lax.all_gather(shard_low, "zero", axis=1, tiled=True),
-        lax.all_gather(norm_params.astype(jnp.bfloat16), "zero", axis=1, tiled=True),
+        gather_by_bits(norm_params.astype(jnp.bfloat16), "zero", 1),
     )
     norm_gains = norm_whole.astype(jnp.float32)
     slopes = jnp.asarray(alibi_slopes(head_count))

time: 1720 us -> 1720 us (level)
  blocking collectives: 282 us -> 238 us
  waiting for transfers between devices: 937 us -> 972 us
    all_gather x1 -> x0, blocking collectives: 43.7 us -> none  [shards(): lax.all_gather(norm_params.astype(jnp.bfloat16), 'zero', axis=1, tiled=True)]
    all_gather x1, waiting for transfers between devices: 150 us -> 182 us  [shards(): lax.all_gather(shard_low, 'zero', axis=1, tiled=True)]
  transfers between devices with their start and end apart: 6 -> 10, of which waited for: 5 -> 7; matrix products, arithmetic and copies ran while one was open for 4% -> 4% of each run, Pallas kernels for 0% -> 0%
where the time goes in v1:
time: 1720 us; the launch traced here: 1710 us
  waiting for transfers between devices  972 us (57%)
  blocking collectives  238 us (14%)
  matrix products  194 us (11%)
  local copies, waits for them, and re-layouts  171 us (10%)
  other arithmetic  94.6 us (6%)
  starting transfers between devices  24.5 us (1%)
    reduce_scatter x1, waiting for transfers between devices, shards(): lax.psum_scatter(tile_grads, 'zero', scatter_dimension=1, tiled=True)  539 us
    unnamed x5, waiting for transfers between devices  209 us
    all_gather x1, waiting for transfers between devices, shards(): lax.all_gather(shard_low, 'zero', axis=1, tiled=True)  182 us
    all_to_all x1, blocking collectives, shards(): lax.all_to_all(outgoing(left_basis), 'zero', split_axis=0, concat_axis=2,...  62.3 us
    all_to_all x1, blocking collectives, shards(): lax.all_to_all(outgoing(first_moment), 'zero', split_axis=0, concat_axis=...  57.8 us
    all_to_all x1, blocking collectives, shards(): lax.all_to_all(outgoing(tile_sum), 'zero', split_axis=0, concat_axis=2, t...  57.8 us
    all_to_all x1, blocking collectives, shards(): lax.all_to_all(outgoing(second_moment), 'zero', split_axis=0, concat_axis...  57.7 us
    concatenate x1, local copies, waits for them, and re-layouts, shards(): jnp.concatenate([grad_qkv, grad_out[None], grad_gate_up, grad_down], axis=0)  37.9 us
  transfers between devices with their start and end apart: 10, of which 7 were waited for; matrix products, arithmetic and copies ran while one was open for 4% of the time, Pallas kernels for 0%

profile of v1, /device:TPU:0, one launch (start us, length us, event | category | flops | bytes accessed | tf_op | source)
XLA Modules:
  0.0 1709.3 jit_solution(2418287397995983281)
XLA Ops:
  16.1 9.2 gather_fusion
  43.0 182.2 %all-gather.2.cloned.1.call-done = bf16[16,768,768]{2,1,0:T(8,128)(2,1)} async-done(((bf16[16,48,768]{2,1,0:T(8,128)(2,1)}), bf16[16,768,768]{2,1,0:T(8,128)(2,1)}) %all-gather.2.cloned.1.call-update) | async-done | bytes 18874384 | tf_op jit(solution)/shard_map/all_gather | solution.py:98
  225.2 6.4 convert_bitcast_fusion
  261.0 19.5 %fusion.9 = f32[1024,8,768]{2,0,1:T(8,128)} fusion(bf16[16,768,768]{2,1,0:T(8,128)(2,1)} %all-gather.2.cloned.1.call-done, f32[1024,768]{0,1:T(8,128)S(1)} %get-tuple-element.109, f32[768]{0:T(1024)S(1)} %add.145, f32[768]{0:T(1024)S(1)} %mul.298, f32[1024]{0:T(1024)S(1)} %fusion.81, f32[1024]{0:T(1024)S(1)} %broadcast_multiply_fusion.4), kind=kOutput, calls=%fused_computation.31 | convolution fusion | flops 9667608576 | bytes 37763072 | tf_op jit(solution)/shard_map/td,fde->tfe/dot_general | solution.py:129
  280.4 29.9 %multiply_convert_fusion.1 = (bf16[1024,4,768]{2,0,1:T(8,128)(2,1)S(1)}, f32[1024,4,768]{2,0,1:T(8,128)}) fusion(f32[1024,8,768]{2,0,1:T(8,128)} %fusion.9), kind=kLoop, calls=%fused_computation.13 | loop fusion | flops 207618048 | bytes 44040192 | tf_op jit(solution)/shard_map/convert_element_type | solution.py:138
  310.4 9.3 fusion.103
  324.2 24.4 %add_convert_fusion = (bf16[1024,4,768]{2,0,1:T(8,128)(2,1)}, bf16[1024,4,768]{2,0,1:T(8,128)(2,1)}) fusion(f32[1024,4,768]{2,0,1:T(8,128)} %get-tuple-element.84, f32[1024,8,768]{2,0,1:T(8,128)} %fusion.9, bf16[16,768,768]{2,1,0:T(8,128)(2,1)} %all-gather.2.cloned.1.call-done, f32[1024]{0:T(1024)S(1)} %negate_multiply_fusion.2, ...), kind=kOutput, calls=%fused_computation.12 | convolution fusion | flops 4895539200 | bytes 59788288 | tf_op jit(solution)/shard_map/td,fed->tfe/dot_general | solution.py:150
  348.6 24.5 %multiply_reduce_fusion.1 = (f32[768]{0:T(1024)}, f32[1024]{0:T(1024)S(1)}, f32[768]{0:T(1024)}, f32[1024,768]{0,1:T(8,128)}) fusion(f32[1024,768]{0,1:T(8,128)} %copy-done.12, f32[1024]{0:T(1024)S(1)} %fusion.81, f32[1024]{0:T(1024)S(1)} %broadcast_multiply_fusion.4, f32[768]{0:T(1024)S(1)} %mul.298, ...), kind=kOutput, calls=%fused_computation.65 | convolution fusion | flops 9683334144 | bytes 33071104 | tf_op jit(solution)/shard_map/tfe,fde->td/dot_general | solution.py:164
  387.2 5.2 fusion.57
  405.7 8.2 fusion.77
  413.9 18.5 %fusion.12 = f32[8,768,768]{1,2,0:T(8,128)} fusion(bf16[1024,4,768]{2,0,1:T(8,128)(2,1)} %get-tuple-element.86, bf16[1024,4,768]{2,0,1:T(8,128)(2,1)} %get-tuple-element.85, f32[1024,768]{0,1:T(8,128)} %copy-done.12, f32[768]{0:T(1024)S(1)} %add.145, f32[768]{0:T(1024)S(1)} %mul.298, f32[1024]{0:T(1024)S(1)} %fusion.81, f32[1024]{0:T(1024)S(1)} %broadcast_multiply_fusion.4), kind=kOutput, calls=%fused_computation.34 | convolution fusion | flops 9673900032 | bytes 34617344 | tf_op jit(solution)/shard_map/td,tfe->fde/dot_general | solution.py:161
  432.4 5.2 convolution_bitcast_fusion.2
  466.6 9.7 convolution_bitcast_fusion
  476.3 25.9 %pad_maximum_fusion = f32[16,768,768]{1,2,0:T(8,128)} fusion(f32[4,768,768]{1,2,0:T(8,128)} %fusion.77, f32[8,768,768]{1,2,0:T(8,128)} %fusion.12, f32[1,768,768]{1,2,0:T(8,128)} %convolution_bitcast_fusion.2, f32[3,768,768]{1,2,0:T(8,128)} %convolution_bitcast_fusion), kind=kLoop, calls=%fused_computation.7 | loop fusion | flops 28311552 | bytes 75497472 | tf_op jit(solution)/shard_map/concatenate | solution.py:199
  502.2 37.9 %copy.279 = f32[16,768,768]{2,0,1:T(8,128)} copy(f32[16,768,768]{1,2,0:T(8,128)} %pad_maximum_fusion) | data formatting | bytes 75497472 | tf_op jit(solution)/shard_map/concatenate | solution.py:199
  540.3 539.0 %reduce-scatter.5.cloned.1.call-done = f32[16,48,768]{2,0,1:T(8,128)} async-done(((f32[16,768,768]{2,0,1:T(8,128)}), f32[16,48,768]{2,0,1:T(8,128)}) %reduce-scatter.5.cloned.1.call-update) | async-done | bytes 2359312 | tf_op jit(solution)/shard_map/reduce_scatter | solution.py:219
  1097.3 7.6 all-reduce.2.cloned.1.call-done
  1108.7 7.8 select_bitcast_fusion
  1116.5 62.3 %all_to_all.60 = f32[16,1,48,768]{3,2,1,0:T(8,128)} all-to-all(f32[16,1,48,768]{3,2,1,0:T(8,128)} %get-tuple-element.102), channel_id=1, replica_groups=mesh['dp'=2,'zero'=16] {'zero'}, dimensions={0} | all-to-all | bytes 4718592 | tf_op jit(solution)/shard_map/all_to_all | solution.py:223
  1178.8 57.7 %all_to_all.61 = f32[16,1,48,768]{3,2,1,0:T(8,128)} all-to-all(f32[16,1,48,768]{3,2,1,0:T(8,128)S(1)} %get-tuple-element.101), channel_id=1, replica_groups=mesh['dp'=2,'zero'=16] {'zero'}, dimensions={0} | all-to-all | bytes 4718592 | tf_op jit(solution)/shard_map/all_to_all | solution.py:243
  1236.5 57.8 %all_to_all.62 = f32[16,1,48,768]{3,2,1,0:T(8,128)} all-to-all(f32[16,1,48,768]{3,2,1,0:T(8,128)S(1)} %get-tuple-element.105), channel_id=1, replica_groups=mesh['dp'=2,'zero'=16] {'zero'}, dimensions={0} | all-to-all | bytes 4718592 | tf_op jit(solution)/shard_map/all_to_all | solution.py:238
  1294.4 57.8 %all_to_all.63 = f32[16,1,48,768]{3,2,1,0:T(8,128)} all-to-all(f32[16,1,48,768]{3,2,1,0:T(8,128)S(1)} %get-tuple-element.103), channel_id=1, replica_groups=mesh['dp'=2,'zero'=16] {'zero'}, dimensions={0} | all-to-all | bytes 4718592 | tf_op jit(solution)/shard_map/all_to_all | solution.py:232
  1364.4 7.7 fusion.37
  1372.1 31.2 %all-to-all-done.3 = f32[16,1,48,768]{3,2,1,0:T(8,128)} async-done(((f32[16,1,48,768]{3,2,1,0:T(8,128)}), f32[16,1,48,768]{3,2,1,0:T(8,128)}, u32[]{:S(2)}, u32[]{:S(2)}) %all-to-all-start.3) | async-done | bytes 2359328 | tf_op jit(solution)/shard_map/all_to_all | solution.py:226
  1403.3 10.2 fusion.31
  1413.5 6.5 fusion.40
  1420.1 7.9 convolution_bitcast_fusion.1
  1428.4 10.4 copy.282
  1438.8 10.9 all-to-all-start.5
  1450.9 10.0 fusion.23
  1467.0 209.3 %reduce-scatter.7.cloned.1.call-done = f32[48,4]{1,0:T(8,128)} async-done(((f32[768,4]{1,0:T(8,128)}), f32[48,4]{1,0:T(8,128)}) %reduce-scatter.7.cloned.1.call-update) | async-done | bytes 784
  1687.2 6.9 gather_fusion.1
  (196 shorter events, 176.4 us)
Async XLA Ops:
  7.2 1076.6 %copy-start = (f32[16,48,768]{2,1,0:T(8,128)S(1)}, f32[16,48,768]{2,1,0:T(8,128)}, u32[]{:S(2)}) copy-start(f32[16,48,768]{2,1,0:T(8,128)} %param.25) | copy-start | bytes 7077892
  7.2 8.7 copy-start.27
  7.2 8.7 copy-start.24
  7.2 218.0 %all-gather.2.cloned.1.call-start = ((), (), s32[]{:S(2)}) async-start(), calls=%async_computation.8 | async-start | bytes 20054016 | tf_op jit(solution)/shard_map/all_gather | solution.py:98
  10.2 1069.1 %reduce-scatter.5.cloned.1.call-start = ((), (), s32[]{:S(2)}) async-start(), calls=%async_computation.9 | async-start | bytes 40108032 | tf_op jit(solution)/shard_map/reduce_scatter | solution.py:219
  10.3 17.7 %collective-permute-start = (bf16[1,4,48]{2,1,0:T(4,128)(2,1)S(1)}, bf16[1,4,48]{2,1,0:T(4,128)(2,1)S(1)}, u32[]{:S(2)}, u32[]{:S(2)}) collective-permute-start(bf16[1,4,48]{2,1,0:T(4,128)(2,1)S(1)} %get-tuple-element.100), channel_id=1, source_target_pairs={{0,1},{1,0},{2,3},{3,2},{4,5},{5,4},{6,7},{7,6},{8,9},{9,8},{10,11... | collective-permute-start | bytes 1160 | tf_op jit(solution)/shard_map/ppermute | solution.py:32
  27.8 11.6 copy-start.34
  28.0 9.1 copy-start.30
  28.0 4.8 collective-permute-start.1
  32.8 4.1 collective-permute-start.2
  37.0 5.5 collective-permute-start.3
  260.5 49.8 %copy-start.12 = (f32[1024,768]{0,1:T(8,128)}, f32[1024,768]{0,1:T(8,128)S(1)}, u32[]{:S(2)}) copy-start(f32[1024,768]{0,1:T(8,128)S(1)} %get-tuple-element.109) | copy-start | bytes 9437188
  310.4 9.4 copy-start.15
  310.4 9.4 copy-start.6
  387.2 5.2 copy-start.9
  387.2 9.8 slice-start
  392.4 4.6 slice-start.1
  392.4 12.5 slice-start.2
  397.0 7.8 slice-start.3
  540.2 564.7 %all-reduce.2.cloned.1.call-start = ((), (), s32[]{:S(2)}) async-start(), calls=%async_computation.10 | async-start | bytes 4718592 | tf_op jit(solution)/shard_map/psum | solution.py:222
  1352.1 51.1 %all-to-all-start.3 = ((f32[16,1,48,768]{3,2,1,0:T(8,128)}), f32[16,1,48,768]{3,2,1,0:T(8,128)}, u32[]{:S(2)}, u32[]{:S(2)}) async-start(f32[16,1,48,768]{3,2,1,0:T(8,128)} %get-tuple-element.104), calls=%async_computation.4 | async-start | bytes 4718592 | tf_op jit(solution)/shard_map/all_to_all | solution.py:226
  1403.2 10.2 copy-start.18
  1438.8 11.0 copy-start.23
  1438.8 11.0 copy-start.22
  1438.8 11.0 copy-start.29
  1438.8 11.1 copy-start.28
  1438.8 12.1 copy-start.31
  1438.8 241.4 %all-to-all-start.5 = ((f32[1,1,3,768,768]{4,1,2,0,3:T(1,128)}), f32[1,1,3,768,768]{4,1,2,0,3:T(1,128)}, u32[]{:S(2)}, u32[]{:S(2)}) async-start(f32[1,1,3,768,768]{4,1,2,0,3:T(1,128)} %copy.282), calls=%async_computation.6 | async-start | bytes 14155776 | tf_op jit(solution)/shard_map/all_to_all | solution.py:250
  1449.7 226.6 %reduce-scatter.7.cloned.1.call-start = ((), (), s32[]{:S(2)}) async-start(), calls=%async_computation.11 | async-start | bytes 417792
  1463.4 216.1 %copy-start.26 = (f32[4,48]{1,0:T(4,128)S(1)}, f32[4,48]{1,0:T(4,128)}, u32[]{:S(2)}) copy-start(f32[4,48]{1,0:T(4,128)} %param.23) | copy-start | bytes 2308
  1463.4 216.1 %copy-start.32 = (f32[4,48]{1,0:T(4,128)S(1)}, f32[4,48]{1,0:T(4,128)}, u32[]{:S(2)}) copy-start(f32[4,48]{1,0:T(4,128)} %param.29) | copy-start | bytes 2308
  1463.4 216.1 %copy-start.33 = (f32[4,48]{1,0:T(4,128)S(1)}, f32[4,48]{1,0:T(4,128)}, u32[]{:S(2)}) copy-start(f32[4,48]{1,0:T(4,128)} %param.28) | copy-start | bytes 2308
  (17 other events, 46.1 us)
Sparse Core Ops, SparseCore 0:
  11.3 213.8 all-gather.1
  540.3 538.9 reduce-scatter.4
  1083.9 20.9 all-reduce.1
  1455.4 220.8 reduce-scatter.6
